TPU v7x, 32 devices: a whole 2x2x4 slice. The times are simulated.
32 devices in a mesh: groups: 2 (over y), dom: 4 (over z), ens: 4 (over x, core).
Axes of the slice: x: 2, y: 2, z: 4, core: 2. Of those that a mesh axis runs over, the one named last changes fastest.
Arguments:
- state: float32 [16, 256, 512], P('ens', ('groups', 'dom')), parts along dimension 1, may hold values from -8 to 8, as said below
- coords: float32 [3, 2048], P(None, ('groups', 'dom')), parts along dimension 1, may hold values from -1 to 1
- owner_local: int32 [2048], P(('groups', 'dom')), parts along dimension 0, may hold values from 0 to 31
- counts: int32 [8, 4], P(('groups', 'dom')), parts along dimension 0, may hold values from 32 to 64, as said below
- obs_value: float32 [2048], P(('groups', 'dom')), parts along dimension 0, may hold values from 0.5 to 3.5
- obs_weight: float32 [2048], P(('groups', 'dom')), parts along dimension 0, as said below
Outputs:
- analysis: float32 [16, 256, 512], P('ens', ('groups', 'dom')), parts along dimension 1
There are 2 independent parts, one for each index of `groups`. A program takes and returns all parts, laid end to end along the dimension named above; each array names one. Nothing has to cross between parts.
Inputs may be any that keep to these rules, and one draw needn't show every extreme that they name: `state`: each member is an independent field plus an offset of its own. The sensors of one block are stored in order of owner block: the first counts[d, 0] slots belong to owner block 0, the next counts[d, 1] to block 1, and so on; slots after the last of them are unused. For one owner block, chosen by the draw, every row holds exactly 64. `obs_weight`: Positive.
All inputs are finite; a program needn't handle non-finite values.
Results may differ from a plain program's by a relative error of at most 0.00028.
Values sent between devices are 32-bit elements; how exact they have to be, the bound alone decides.
No kernel may reach another device: no remote copies, remote signals or barrier semaphores. Data moves between devices by JAX's collectives and lax.ppermute only.
A program may use at most 64 MiB of HBM per device.

v0:
```python
import jax
import jax.numpy as jnp
from jax import lax
from jax.sharding import PartitionSpec as P

CAP = 64
NS_ITERS = 8
GLL_POINTS = (
    -1.0,
    -0.8717401485096066,
    -0.5917001814331423,
    -0.2092992179024789,
    0.2092992179024789,
    0.5917001814331423,
    0.8717401485096066,
    1.0,
)
INFLATION = 1.1


def lagrange(position):
    basis_rows = []
    for node_index in range(8):
        product = jnp.ones_like(position)
        for other_node in range(8):
            if other_node != node_index:
                product = (
                    product
                    * (position - GLL_POINTS[other_node])
                    / (GLL_POINTS[node_index] - GLL_POINTS[other_node])
                )
        basis_rows.append(product)
    return jnp.stack(basis_rows, 0)


def node_weights(sensor_coords):
    along_r = lagrange(sensor_coords[0]).T
    along_s = lagrange(sensor_coords[1]).T
    along_t = lagrange(sensor_coords[2]).T
    node_table = along_t[:, :, None, None] * along_s[:, None, :, None] * along_r[:, None, None, :]
    return node_table.reshape(sensor_coords.shape[1], 512)


def analysis_weights(cross_terms, project):
    highest = lax.Precision.HIGHEST
    members = cross_terms.shape[0]
    identity = jnp.eye(members, dtype=jnp.float32)
    system = cross_terms + (members - 1) / INFLATION * identity
    trace_value = jnp.trace(system)
    iterate = system / trace_value
    inverse_root = identity
    for sweep in range(NS_ITERS):
        middle = 0.5 * (3.0 * identity - jnp.dot(inverse_root, iterate, precision=highest))
        iterate = jnp.dot(iterate, middle, precision=highest)
        inverse_root = jnp.dot(middle, inverse_root, precision=highest)
    mean_weights = (
        jnp.dot(inverse_root, jnp.dot(inverse_root, project, precision=highest), precision=highest)
        / trace_value
    )
    transform = inverse_root * jnp.sqrt((members - 1) / trace_value) + mean_weights[:, None]
    return transform - jnp.mean(transform, axis=0, keepdims=True) + 1.0 / members


def on_device(state, coords, owner_local, counts, obs_value, obs_weight):
    highest = lax.Precision.HIGHEST
    local_members, local_elements, node_count = state.shape
    row_counts = counts[0]
    starts = jnp.cumsum(row_counts) - row_counts
    column = jnp.arange(CAP, dtype=jnp.int32)
    in_use = column[None, :] < row_counts[:, None]
    slot_index = jnp.minimum(starts[:, None] + column[None, :], coords.shape[1] - 1)
    tile_coords = coords[:, slot_index]
    tile_owner = owner_local[slot_index][None]
    tile_obs = obs_value[slot_index]
    tile_weight = jnp.where(in_use, obs_weight[slot_index], jnp.zeros_like(tile_obs))
    node_major = state.transpose(2, 0, 1).reshape(node_count, local_members * local_elements)
    element_ids = jnp.arange(local_elements, dtype=jnp.int32)
    sensor_coords = lax.all_to_all(tile_coords, "dom", split_axis=1, concat_axis=1, tiled=True)
    sources = sensor_coords.shape[1]
    item_count = sensor_coords.shape[2]
    node_table = node_weights(sensor_coords.reshape(3, sources * item_count))
    partial_values = jnp.dot(node_table, node_major, precision=highest)
    partial_values = partial_values.reshape(sources * item_count, local_members, local_elements)
    selector = (
        lax.all_to_all(tile_owner, "dom", split_axis=1, concat_axis=1, tiled=True).reshape(
            sources * item_count, 1
        )
        == element_ids[None, :]
    ).astype(jnp.float32)
    chosen = jnp.sum(partial_values * selector[:, None, :], axis=2)
    owner_values = chosen.T.reshape(local_members, sources, item_count)
    member_part = lax.all_to_all(owner_values, "dom", split_axis=1, concat_axis=1, tiled=True)
    all_values = lax.all_gather(member_part, "ens", axis=0, tiled=True)
    members = all_values.shape[0]
    flat_values = all_values.reshape(members, -1)
    mean_value = jnp.mean(flat_values, axis=0)
    anomaly = flat_values - mean_value[None, :]
    weighted = anomaly * tile_weight.reshape(-1)[None, :]
    cross_terms = jnp.dot(weighted, anomaly.T, precision=highest)
    project = jnp.dot(weighted, tile_obs.reshape(-1) - mean_value, precision=highest)
    cross_terms, project = lax.psum((cross_terms, project), "dom")
    mixing = analysis_weights(cross_terms, project)
    grouped = lax.all_to_all(state, "ens", split_axis=1, concat_axis=0, tiled=True)
    member_total = grouped.shape[0]
    mixed = jnp.dot(mixing.T, grouped.reshape(member_total, -1), precision=highest).reshape(
        grouped.shape
    )
    return lax.all_to_all(mixed, "ens", split_axis=0, concat_axis=1, tiled=True)


def solution(mesh):
    return jax.shard_map(
        on_device,
        mesh=mesh,
        in_specs=(
            P("ens", ("groups", "dom"), None),
            P(None, ("groups", "dom")),
            P(("groups", "dom")),
            P(("groups", "dom"), None),
            P(("groups", "dom")),
            P(("groups", "dom")),
        ),
        out_specs=P("ens", ("groups", "dom"), None),
        check_vma=False,
    )
```

profile of v0, /device:TPU:0, one launch (start us, length us, event | category | flops | bytes accessed | tf_op | source)
XLA Modules:
  0.0 76.4 jit_solution(562660524366019711)
XLA Ops:
  0.0 0.7 copy-done.5
  0.7 0.2 reduce-window.8
  0.9 0.1 reshape.2092
  1.0 1.9 %gather_fusion.1 = s32[256]{0:T(256)S(1)} fusion(s32[256]{0:T(256)S(1)} %copy-done, s32[1024]{0:T(1024)S(1)} %pad_clamp_fusion), kind=kCustom, calls=%fused_computation.1 | custom fusion | bytes 3072 | tf_op jit(solution)/shard_map/gather | solution.py:73
  3.0 0.7 broadcast_in_dim.5
  3.7 6.3 %all-to-all-start.1 = ((s32[1,4,64]{2,0,1:T(1,128)}), s32[1,4,64]{2,0,1:T(1,128)S(1)}, u32[]{:S(2)}, u32[]{:S(2)}) async-start(s32[1,4,64]{2,0,1:T(1,128)} %broadcast_in_dim.5), calls=%async_computation.1 | async-start | bytes 4096 | tf_op jit(solution)/shard_map/all_to_all | solution.py:85
  10.0 0.1 copy.35
  10.2 0.7 gather_fusion
  10.9 0.1 copy.36
  11.0 0.7 reshape.2397
  11.7 1.9 %gather_fusion.2 = f32[256]{0:T(256)S(1)} fusion(f32[256]{0:T(256)S(1)} %copy-done.1, s32[1024]{0:T(1024)S(1)} %pad_clamp_fusion), kind=kCustom, calls=%fused_computation.2 | custom fusion | bytes 3072 | tf_op jit(solution)/shard_map/gather | solution.py:75
  13.7 1.7 %all-to-all-done.1 = s32[1,4,64]{2,0,1:T(1,128)S(1)} async-done(((s32[1,4,64]{2,0,1:T(1,128)}), s32[1,4,64]{2,0,1:T(1,128)S(1)}, u32[]{:S(2)}, u32[]{:S(2)}) %all-to-all-start.1) | async-done | bytes 1056 | tf_op jit(solution)/shard_map/all_to_all | solution.py:85
  15.4 3.4 %all-to-all-start = ((f32[4,1,192]{2,1,0:T(1,128)}), f32[4,1,192]{2,1,0:T(1,128)S(1)}, u32[]{:S(2)}, u32[]{:S(2)}) async-start(f32[4,1,192]{2,1,0:T(1,128)} %reshape.2397), calls=%async_computation | async-start | bytes 8192 | tf_op jit(solution)/shard_map/all_to_all | solution.py:78
  18.8 0.6 broadcast.3262
  19.4 0.7 reduce.4
  20.1 0.1 eq.47
  20.2 4.2 %all-to-all-done = f32[4,1,192]{2,1,0:T(1,128)S(1)} async-done(((f32[4,1,192]{2,1,0:T(1,128)}), f32[4,1,192]{2,1,0:T(1,128)S(1)}, u32[]{:S(2)}, u32[]{:S(2)}) %all-to-all-start) | async-done | bytes 3104 | tf_op jit(solution)/shard_map/all_to_all | solution.py:78
  24.4 0.5 broadcast.3265
  24.9 0.6 reduce.5
  27.8 0.9 %copy-done.3 = f32[4,32,512]{2,1,0:T(8,128)S(1)} copy-done((f32[4,32,512]{2,1,0:T(8,128)S(1)}, f32[4,32,512]{2,1,0:T(8,128)}, u32[]{:S(2)}) %copy-start.3) | copy-done | bytes 262168
  28.7 0.5 fusion
  29.2 0.7 reshape.2399
  29.9 3.2 %all-to-all-start.2 = ((f32[4,1,256]{2,1,0:T(1,128)}), f32[4,1,256]{2,1,0:T(1,128)S(1)}, u32[]{:S(2)}, u32[]{:S(2)}) async-start(f32[4,1,256]{2,1,0:T(1,128)} %reshape.2399), calls=%async_computation.2 | async-start | bytes 8192 | tf_op jit(solution)/shard_map/all_to_all | solution.py:92
  33.2 0.9 %copy.45 = f32[4,32,512]{2,0,1:T(4,128)} copy(f32[4,32,512]{2,1,0:T(8,128)S(1)} %copy-done.3) | data formatting | bytes 524288 | tf_op args[0]
  34.1 1.9 %gather_fusion.3 = f32[256]{0:T(256)S(1)} fusion(f32[256]{0:T(256)S(1)} %copy-done.2, s32[1024]{0:T(1024)S(1)} %pad_clamp_fusion), kind=kCustom, calls=%fused_computation.3 | custom fusion | bytes 3072 | tf_op jit(solution)/shard_map/gather | solution.py:74
  36.1 2.6 %all-to-all-done.2 = f32[4,1,256]{2,1,0:T(1,128)S(1)} async-done(((f32[4,1,256]{2,1,0:T(1,128)}), f32[4,1,256]{2,1,0:T(1,128)S(1)}, u32[]{:S(2)}, u32[]{:S(2)}) %all-to-all-start.2) | async-done | bytes 4128 | tf_op jit(solution)/shard_map/all_to_all | solution.py:92
  38.7 3.4 %all-to-all-start.3 = ((f32[4,32,512]{2,0,1:T(4,128)}), f32[4,32,512]{2,0,1:T(4,128)S(1)}, u32[]{:S(2)}, u32[]{:S(2)}) async-start(f32[4,32,512]{2,0,1:T(4,128)} %copy.45), calls=%async_computation.3 | async-start | bytes 524288 | tf_op jit(solution)/shard_map/all_to_all | solution.py:103
  42.1 0.6 reduce.6
  42.7 0.1 reshape.2400
  42.8 6.3 %all_gather.3 = f32[16,4,64]{2,1,0:T(4,128)S(1)} all-gather(f32[4,4,64]{2,1,0:T(4,128)S(1)} %copy.42), channel_id=1, replica_groups=mesh['groups'=2,'dom'=4,'ens'=4] {'ens'}, dimensions={0}, use_global_device_ids=true | all-gather | bytes 20480 | tf_op jit(solution)/shard_map/all_gather | solution.py:93
  49.2 0.1 convolution_bitcast_fusion.1
  49.3 0.2 convolution_bitcast_fusion
  49.5 9.9 %all-reduce = (f32[16,16]{1,0:T(8,128)S(1)}, f32[16]{0:T(128)S(1)}) all-reduce(f32[16,16]{1,0:T(8,128)S(1)} %convolution_bitcast_fusion, f32[16]{0:T(128)S(1)} %convolution_bitcast_fusion.1), channel_id=1, replica_groups=mesh['groups'=2,'dom'=4,'ens'=4] {'dom'}, use_global_device_ids=true, to_apply=%region_3.4 | all-reduce | flops 272 | bytes 2176 | tf_op jit(solution)/shard_map/psum | solution.py:101
  59.4 0.7 select_reduce_fusion
  60.1 0.8 %fusion.8 = f32[16,16]{1,0:T(8,128)S(1)} fusion(f32[16,16]{1,0:T(8,128)S(1)} %get-tuple-element.5, f32[]{:T(128)} %select_reduce_fusion), kind=kOutput, calls=%fused_computation.21 | convolution fusion | flops 51456 | bytes 2052 | tf_op jit(solution)/shard_map/dot_general | solution.py:53
  60.9 0.8 %fusion.28 = f32[16,16]{1,0:T(8,128)S(1)} fusion(f32[16,16]{1,0:T(8,128)S(1)} %fusion.8, f32[16,16]{1,0:T(8,128)S(1)} %get-tuple-element.5, f32[]{:T(128)} %select_reduce_fusion), kind=kOutput, calls=%fused_computation.82 | convolution fusion | flops 50176 | bytes 3076 | tf_op jit(solution)/shard_map/dot_general | solution.py:54
  61.8 0.1 fusion.20
  61.9 0.1 fusion.7
  62.0 0.1 fusion.40
  62.2 0.1 fusion.39
  62.3 0.1 fusion.6
  62.4 0.1 fusion.42
  62.6 0.1 fusion.41
  62.7 0.1 fusion.5
  62.8 0.1 fusion.44
  63.0 0.1 fusion.43
  63.1 0.1 fusion.4
  63.3 0.1 fusion.46
  63.4 0.1 fusion.45
  63.5 0.1 fusion.3
  63.7 0.1 fusion.48
  63.8 0.1 fusion.47
  64.0 0.1 fusion.2
  64.1 0.1 fusion.50
  64.2 0.1 fusion.49
  64.4 0.1 fusion.1
  64.5 0.1 fusion.51
  64.7 0.1 convolution_bitcast_fusion.3
  64.8 0.8 %fusion.9 = f32[16]{0:T(128)S(1)} fusion(f32[16,16]{1,0:T(8,128)S(1)} %fusion.51, f32[16,1]{0,1:T(1,128)S(1)} %convolution_bitcast_fusion.3, f32[]{:T(128)} %select_reduce_fusion), kind=kOutput, calls=%fused_computation.26 | convolution fusion | flops 3088 | bytes 1156 | tf_op jit(solution)/shard_map/dot_general | solution.py:57
  66.4 0.1 fusion.21
  66.6 0.6 fusion.10
  67.2 0.2 copy.49
  67.3 8.4 %all_to_all.48 = f32[16,8,512]{2,1,0:T(8,128)S(1)} all-to-all(f32[16,8,512]{2,1,0:T(8,128)S(1)} %copy.49), channel_id=1, replica_groups=mesh['groups'=2,'dom'=4,'ens'=4] {'ens'}, dimensions={0} | all-to-all | bytes 524288 | tf_op jit(solution)/shard_map/all_to_all | solution.py:108
  75.7 0.7 copy.76
  (63 shorter events, 2.8 us)
Async XLA Ops:
  0.0 1.0 %copy-start = (s32[256]{0:T(256)S(1)}, s32[256]{0:T(256)}, u32[]{:S(2)}) copy-start(s32[256]{0:T(256)} %param.8) | copy-start | bytes 3076
  0.0 0.7 copy-start.5
  3.0 7.0 %copy-start.4 = (f32[3,256]{1,0:T(4,128)S(1)}, f32[3,256]{1,0:T(4,128)}, u32[]{:S(2)}) copy-start(f32[3,256]{1,0:T(4,128)} %param.7) | copy-start | bytes 9220
  3.7 11.8 %all-to-all-start.1 = ((s32[1,4,64]{2,0,1:T(1,128)}), s32[1,4,64]{2,0,1:T(1,128)S(1)}, u32[]{:S(2)}, u32[]{:S(2)}) async-start(s32[1,4,64]{2,0,1:T(1,128)} %broadcast_in_dim.5), calls=%async_computation.1 | async-start | bytes 4096 | tf_op jit(solution)/shard_map/all_to_all | solution.py:85
  11.0 0.7 copy-start.1
  15.4 9.0 %all-to-all-start = ((f32[4,1,192]{2,1,0:T(1,128)}), f32[4,1,192]{2,1,0:T(1,128)S(1)}, u32[]{:S(2)}, u32[]{:S(2)}) async-start(f32[4,1,192]{2,1,0:T(1,128)} %reshape.2397), calls=%async_computation | async-start | bytes 8192 | tf_op jit(solution)/shard_map/all_to_all | solution.py:78
  27.7 1.0 %copy-start.3 = (f32[4,32,512]{2,1,0:T(8,128)S(1)}, f32[4,32,512]{2,1,0:T(8,128)}, u32[]{:S(2)}) copy-start(f32[4,32,512]{2,1,0:T(8,128)} %param.6) | copy-start | bytes 786436
  29.9 8.8 %all-to-all-start.2 = ((f32[4,1,256]{2,1,0:T(1,128)}), f32[4,1,256]{2,1,0:T(1,128)S(1)}, u32[]{:S(2)}, u32[]{:S(2)}) async-start(f32[4,1,256]{2,1,0:T(1,128)} %reshape.2399), calls=%async_computation.2 | async-start | bytes 8192 | tf_op jit(solution)/shard_map/all_to_all | solution.py:92
  33.2 0.9 %copy-start.2 = (f32[256]{0:T(256)S(1)}, f32[256]{0:T(256)}, u32[]{:S(2)}) copy-start(f32[256]{0:T(256)} %param.10) | copy-start | bytes 3076
  38.7 27.8 %all-to-all-start.3 = ((f32[4,32,512]{2,0,1:T(4,128)}), f32[4,32,512]{2,0,1:T(4,128)S(1)}, u32[]{:S(2)}, u32[]{:S(2)}) async-start(f32[4,32,512]{2,0,1:T(4,128)} %copy.45), calls=%async_computation.3 | async-start | bytes 524288 | tf_op jit(solution)/shard_map/all_to_all | solution.py:103
where the time goes:
time: 77 us; the launch traced here: 76.4 us
  blocking collectives  24.7 us (32%)
  starting transfers between devices  16.4 us (21%)
  local copies, waits for them, and re-layouts  16 us (21%)
  waiting for transfers between devices  8.47 us (11%)
  matrix products  6.82 us (9%)
  other arithmetic  3.14 us (4%)
  between operations  0.98 us (1%)
    psum x1, blocking collectives, on_device(): cross_terms, project = lax.psum((cross_terms, project), 'dom')  9.93 us
    all_to_all x1, blocking collectives, on_device(): return lax.all_to_all(mixed, 'ens', split_axis=0, concat_axis=1, tiled=True)  8.39 us
    all_to_all x1, starting transfers between devices, on_device(): lax.all_to_all(tile_owner, 'dom', split_axis=1, concat_axis=1, tiled=True)  6.35 us
    all_gather x1, blocking collectives, on_device(): all_values = lax.all_gather(member_part, 'ens', axis=0, tiled=True)  6.34 us
    all_to_all x1, waiting for transfers between devices, on_device(): lax.all_to_all(tile_coords, 'dom', split_axis=1, concat_axis=1, tiled=True)  4.19 us
    unnamed x21, local copies, waits for them, and re-layouts  4.14 us
    all_to_all x1, starting transfers between devices, on_device(): lax.all_to_all(state, 'ens', split_axis=1, concat_axis=0, tiled=True)  3.41 us
    all_to_all x1, starting transfers between devices, on_device(): lax.all_to_all(tile_coords, 'dom', split_axis=1, concat_axis=1, tiled=True)  3.38 us
  transfers between devices with their start and end apart: 4, of which 3 were waited for; matrix products, arithmetic and copies ran while one was open for 20% of the time, Pallas kernels for 0%

commit v1 on v0

--- a/solution.py
+++ b/solution.py
@@ -89,7 +89,12 @@
     ).astype(jnp.float32)
     chosen = jnp.sum(partial_values * selector[:, None, :], axis=2)
     owner_values = chosen.T.reshape(local_members, sources, item_count)
-    member_part = lax.all_to_all(owner_values, "dom", split_axis=1, concat_axis=1, tiled=True)
+    member_part = jnp.concatenate(
+        lax.all_to_all(
+            jnp.stack(jnp.split(owner_values, lax.axis_size("dom"), axis=1)), "dom", 0, 0
+        ),
+        axis=1,
+    )
     all_values = lax.all_gather(member_part, "ens", axis=0, tiled=True)
     members = all_values.shape[0]
     flat_values = all_values.reshape(members, -1)

time: 77 us -> 77 us (level)
    unnamed x21 -> x19, local copies, waits for them, and re-layouts: 4.14 us -> 4.13 us
where the time goes in v1:
time: 77 us; the launch traced here: 76.4 us
  blocking collectives  24.7 us (32%)
  starting transfers between devices  16.4 us (21%)
  local copies, waits for them, and re-layouts  16 us (21%)
  waiting for transfers between devices  8.47 us (11%)
  matrix products  6.82 us (9%)
  other arithmetic  3.16 us (4%)
  between operations  0.98 us (1%)
    psum x1, blocking collectives, on_device(): cross_terms, project = lax.psum((cross_terms, project), 'dom')  9.93 us
    all_to_all x1, blocking collectives, on_device(): return lax.all_to_all(mixed, 'ens', split_axis=0, concat_axis=1, tiled=True)  8.39 us
    all_to_all x1, starting transfers between devices, on_device(): lax.all_to_all(tile_owner, 'dom', split_axis=1, concat_axis=1, tiled=True)  6.35 us
    all_gather x1, blocking collectives, on_device(): all_values = lax.all_gather(member_part, 'ens', axis=0, tiled=True)  6.33 us
    all_to_all x1, waiting for transfers between devices, on_device(): lax.all_to_all(tile_coords, 'dom', split_axis=1, concat_axis=1, tiled=True)  4.19 us
    unnamed x19, local copies, waits for them, and re-layouts  4.13 us
    all_to_all x1, starting transfers between devices, on_device(): lax.all_to_all(state, 'ens', split_axis=1, concat_axis=0, tiled=True)  3.41 us
    all_to_all x1, starting transfers between devices, on_device(): lax.all_to_all(tile_coords, 'dom', split_axis=1, concat_axis=1, tiled=True)  3.38 us
  transfers between devices with their start and end apart: 4, of which 3 were waited for; matrix products, arithmetic and copies ran while one was open for 20% of the time, Pallas kernels for 0%

profile of v1, /device:TPU:0, one launch (start us, length us, event | category | flops | bytes accessed | tf_op | source)
XLA Modules:
  0.0 76.4 jit_solution(6198394552418331400)
XLA Ops:
  0.0 0.7 copy-done.5
  0.7 0.2 reduce-window.8
  0.9 0.1 reshape.2100
  1.0 1.9 %gather_fusion.1 = s32[256]{0:T(256)S(1)} fusion(s32[256]{0:T(256)S(1)} %copy-done, s32[1024]{0:T(1024)S(1)} %pad_clamp_fusion), kind=kCustom, calls=%fused_computation.1 | custom fusion | bytes 3072 | tf_op jit(solution)/shard_map/gather | solution.py:73
  3.0 0.7 broadcast_in_dim.5
  3.7 6.3 %all-to-all-start.1 = ((s32[1,4,64]{2,0,1:T(1,128)}), s32[1,4,64]{2,0,1:T(1,128)S(1)}, u32[]{:S(2)}, u32[]{:S(2)}) async-start(s32[1,4,64]{2,0,1:T(1,128)} %broadcast_in_dim.5), calls=%async_computation.1 | async-start | bytes 4096 | tf_op jit(solution)/shard_map/all_to_all | solution.py:85
  10.0 0.1 copy.41
  10.2 0.7 gather_fusion
  10.9 0.1 copy.42
  11.0 0.7 reshape.2406
  11.7 1.9 %gather_fusion.2 = f32[256]{0:T(256)S(1)} fusion(f32[256]{0:T(256)S(1)} %copy-done.1, s32[1024]{0:T(1024)S(1)} %pad_clamp_fusion), kind=kCustom, calls=%fused_computation.2 | custom fusion | bytes 3072 | tf_op jit(solution)/shard_map/gather | solution.py:75
  13.7 1.7 %all-to-all-done.1 = s32[1,4,64]{2,0,1:T(1,128)S(1)} async-done(((s32[1,4,64]{2,0,1:T(1,128)}), s32[1,4,64]{2,0,1:T(1,128)S(1)}, u32[]{:S(2)}, u32[]{:S(2)}) %all-to-all-start.1) | async-done | bytes 1056 | tf_op jit(solution)/shard_map/all_to_all | solution.py:85
  15.4 3.4 %all-to-all-start = ((f32[4,1,192]{2,1,0:T(1,128)}), f32[4,1,192]{2,1,0:T(1,128)S(1)}, u32[]{:S(2)}, u32[]{:S(2)}) async-start(f32[4,1,192]{2,1,0:T(1,128)} %reshape.2406), calls=%async_computation | async-start | bytes 8192 | tf_op jit(solution)/shard_map/all_to_all | solution.py:78
  18.8 0.6 broadcast.3262
  19.4 0.7 reduce.5
  20.1 0.1 eq.47
  20.2 4.2 %all-to-all-done = f32[4,1,192]{2,1,0:T(1,128)S(1)} async-done(((f32[4,1,192]{2,1,0:T(1,128)}), f32[4,1,192]{2,1,0:T(1,128)S(1)}, u32[]{:S(2)}, u32[]{:S(2)}) %all-to-all-start) | async-done | bytes 3104 | tf_op jit(solution)/shard_map/all_to_all | solution.py:78
  24.4 0.5 broadcast.3263
  24.9 0.6 reduce.6
  27.8 0.9 %copy-done.3 = f32[4,32,512]{2,1,0:T(8,128)S(1)} copy-done((f32[4,32,512]{2,1,0:T(8,128)S(1)}, f32[4,32,512]{2,1,0:T(8,128)}, u32[]{:S(2)}) %copy-start.3) | copy-done | bytes 262168
  28.7 0.5 fusion
  29.2 0.7 reshape.2408
  29.9 3.2 %all-to-all-start.2 = ((f32[4,1,256]{2,1,0:T(1,128)}), f32[4,1,256]{2,1,0:T(1,128)S(1)}, u32[]{:S(2)}, u32[]{:S(2)}) async-start(f32[4,1,256]{2,1,0:T(1,128)} %reshape.2408), calls=%async_computation.2 | async-start | bytes 8192 | tf_op jit(solution)/shard_map/all_to_all | solution.py:93
  33.2 0.9 %copy.53 = f32[4,32,512]{2,0,1:T(4,128)} copy(f32[4,32,512]{2,1,0:T(8,128)S(1)} %copy-done.3) | data formatting | bytes 524288 | tf_op args[0]
  34.1 1.9 %gather_fusion.3 = f32[256]{0:T(256)S(1)} fusion(f32[256]{0:T(256)S(1)} %copy-done.2, s32[1024]{0:T(1024)S(1)} %pad_clamp_fusion), kind=kCustom, calls=%fused_computation.3 | custom fusion | bytes 3072 | tf_op jit(solution)/shard_map/gather | solution.py:74
  36.1 2.6 %all-to-all-done.2 = f32[4,1,256]{2,1,0:T(1,128)S(1)} async-done(((f32[4,1,256]{2,1,0:T(1,128)}), f32[4,1,256]{2,1,0:T(1,128)S(1)}, u32[]{:S(2)}, u32[]{:S(2)}) %all-to-all-start.2) | async-done | bytes 4128 | tf_op jit(solution)/shard_map/all_to_all | solution.py:93
  38.7 3.4 %all-to-all-start.3 = ((f32[4,32,512]{2,0,1:T(4,128)}), f32[4,32,512]{2,0,1:T(4,128)S(1)}, u32[]{:S(2)}, u32[]{:S(2)}) async-start(f32[4,32,512]{2,0,1:T(4,128)} %copy.53), calls=%async_computation.3 | async-start | bytes 524288 | tf_op jit(solution)/shard_map/all_to_all | solution.py:108
  42.1 0.6 reduce.7
  42.7 0.1 reshape.2409
  42.8 6.3 %all-gather = f32[16,4,1,64]{3,1,2,0:T(4,128)S(1)} all-gather(f32[4,4,1,64]{3,1,2,0:T(4,128)S(1)} %copy.50), channel_id=2, replica_groups=mesh['groups'=2,'dom'=4,'ens'=4] {'ens'}, dimensions={0}, use_global_device_ids=true | all-gather | bytes 20480 | tf_op jit(solution)/shard_map/all_gather | solution.py:98
  49.2 0.1 convolution_bitcast_fusion.1
  49.3 0.2 convolution_bitcast_fusion
  49.5 9.9 %all-reduce = (f32[16,16]{1,0:T(8,128)S(1)}, f32[16]{0:T(128)S(1)}) all-reduce(f32[16,16]{1,0:T(8,128)S(1)} %convolution_bitcast_fusion, f32[16]{0:T(128)S(1)} %convolution_bitcast_fusion.1), channel_id=1, replica_groups=mesh['groups'=2,'dom'=4,'ens'=4] {'dom'}, use_global_device_ids=true, to_apply=%region_3.4 | all-reduce | flops 272 | bytes 2176 | tf_op jit(solution)/shard_map/psum | solution.py:106
  59.4 0.7 select_reduce_fusion
  60.1 0.8 %fusion.8 = f32[16,16]{1,0:T(8,128)S(1)} fusion(f32[16,16]{1,0:T(8,128)S(1)} %get-tuple-element.5, f32[]{:T(128)} %select_reduce_fusion), kind=kOutput, calls=%fused_computation.21 | convolution fusion | flops 51456 | bytes 2052 | tf_op jit(solution)/shard_map/dot_general | solution.py:53
  60.9 0.8 %fusion.28 = f32[16,16]{1,0:T(8,128)S(1)} fusion(f32[16,16]{1,0:T(8,128)S(1)} %fusion.8, f32[16,16]{1,0:T(8,128)S(1)} %get-tuple-element.5, f32[]{:T(128)} %select_reduce_fusion), kind=kOutput, calls=%fused_computation.83 | convolution fusion | flops 50176 | bytes 3076 | tf_op jit(solution)/shard_map/dot_general | solution.py:54
  61.8 0.1 fusion.20
  61.9 0.1 fusion.7
  62.0 0.1 fusion.42
  62.2 0.1 fusion.41
  62.3 0.1 fusion.6
  62.4 0.1 fusion.44
  62.6 0.1 fusion.43
  62.7 0.1 fusion.5
  62.8 0.1 fusion.46
  63.0 0.1 fusion.45
  63.1 0.1 fusion.4
  63.3 0.1 fusion.48
  63.4 0.1 fusion.47
  63.5 0.1 fusion.3
  63.7 0.1 fusion.50
  63.8 0.1 fusion.49
  64.0 0.1 fusion.2
  64.1 0.1 fusion.52
  64.2 0.1 fusion.51
  64.4 0.1 fusion.1
  64.5 0.1 fusion.53
  64.7 0.1 convolution_bitcast_fusion.3
  64.8 0.8 %fusion.9 = f32[16]{0:T(128)S(1)} fusion(f32[16,16]{1,0:T(8,128)S(1)} %fusion.53, f32[16,1]{0,1:T(1,128)S(1)} %convolution_bitcast_fusion.3, f32[]{:T(128)} %select_reduce_fusion), kind=kOutput, calls=%fused_computation.26 | convolution fusion | flops 3088 | bytes 1156 | tf_op jit(solution)/shard_map/dot_general | solution.py:57
  66.4 0.1 fusion.21
  66.6 0.6 fusion.10
  67.2 0.2 copy.57
  67.3 8.4 %all_to_all.48 = f32[16,8,512]{2,1,0:T(8,128)S(1)} all-to-all(f32[16,8,512]{2,1,0:T(8,128)S(1)} %copy.57), channel_id=1, replica_groups=mesh['groups'=2,'dom'=4,'ens'=4] {'ens'}, dimensions={0} | all-to-all | bytes 524288 | tf_op jit(solution)/shard_map/all_to_all | solution.py:113
  75.7 0.7 copy.86
  (63 shorter events, 2.8 us)
Async XLA Ops:
  0.0 1.0 %copy-start = (s32[256]{0:T(256)S(1)}, s32[256]{0:T(256)}, u32[]{:S(2)}) copy-start(s32[256]{0:T(256)} %param.8) | copy-start | bytes 3076
  0.0 0.7 copy-start.5
  3.0 7.0 %copy-start.4 = (f32[3,256]{1,0:T(4,128)S(1)}, f32[3,256]{1,0:T(4,128)}, u32[]{:S(2)}) copy-start(f32[3,256]{1,0:T(4,128)} %param.7) | copy-start | bytes 9220
  3.7 11.8 %all-to-all-start.1 = ((s32[1,4,64]{2,0,1:T(1,128)}), s32[1,4,64]{2,0,1:T(1,128)S(1)}, u32[]{:S(2)}, u32[]{:S(2)}) async-start(s32[1,4,64]{2,0,1:T(1,128)} %broadcast_in_dim.5), calls=%async_computation.1 | async-start | bytes 4096 | tf_op jit(solution)/shard_map/all_to_all | solution.py:85
  11.0 0.7 copy-start.1
  15.4 9.0 %all-to-all-start = ((f32[4,1,192]{2,1,0:T(1,128)}), f32[4,1,192]{2,1,0:T(1,128)S(1)}, u32[]{:S(2)}, u32[]{:S(2)}) async-start(f32[4,1,192]{2,1,0:T(1,128)} %reshape.2406), calls=%async_computation | async-start | bytes 8192 | tf_op jit(solution)/shard_map/all_to_all | solution.py:78
  27.7 1.0 %copy-start.3 = (f32[4,32,512]{2,1,0:T(8,128)S(1)}, f32[4,32,512]{2,1,0:T(8,128)}, u32[]{:S(2)}) copy-start(f32[4,32,512]{2,1,0:T(8,128)} %param.6) | copy-start | bytes 786436
  29.9 8.8 %all-to-all-start.2 = ((f32[4,1,256]{2,1,0:T(1,128)}), f32[4,1,256]{2,1,0:T(1,128)S(1)}, u32[]{:S(2)}, u32[]{:S(2)}) async-start(f32[4,1,256]{2,1,0:T(1,128)} %reshape.2408), calls=%async_computation.2 | async-start | bytes 8192 | tf_op jit(solution)/shard_map/all_to_all | solution.py:93
  33.2 0.9 %copy-start.2 = (f32[256]{0:T(256)S(1)}, f32[256]{0:T(256)}, u32[]{:S(2)}) copy-start(f32[256]{0:T(256)} %param.10) | copy-start | bytes 3076
  38.7 27.8 %all-to-all-start.3 = ((f32[4,32,512]{2,0,1:T(4,128)}), f32[4,32,512]{2,0,1:T(4,128)S(1)}, u32[]{:S(2)}, u32[]{:S(2)}) async-start(f32[4,32,512]{2,0,1:T(4,128)} %copy.53), calls=%async_computation.3 | async-start | bytes 524288 | tf_op jit(solution)/shard_map/all_to_all | solution.py:108
